TPU v7x, 32 devices: a whole 2x2x4 slice. The times are simulated.
32 devices in a mesh: grp: 2 (over y), col: 4 (over z), row: 2 (over x), dir: 2 (over core).
Axes of the slice: x: 2, y: 2, z: 4, core: 2. Of those that a mesh axis runs over, the one named last changes fastest.
Arguments:
- slopes_in: bfloat16 [512, 8192], P(None, ('grp', 'col')), parts along dimension 1, may hold values from -6 to 6
- basis_left: bfloat16 [12, 16, 256, 256], P(('row', 'dir'), 'col'), may hold values from -0.09375 to 0.09375
- basis_right: bfloat16 [12, 16, 256, 256], P(('row', 'dir'), 'col'), may hold values from -0.375 to 0.375
- rank_blocks: int32 [12, 16], P(('row', 'dir'), 'col'), may hold values from 1 to 4
- tile_owner: int32 [16], replicated, may hold values from 0 to 15, each once
- footprint: int32 [4, 4, 4, 2048], P(('row', 'dir')), may hold values from 0 to 767
- trace_weight: float32 [4, 4, 4, 2048], P(('row', 'dir')), may hold values from 0 to 0.5
- fitting: bfloat16 [2048, 4096], P(None, 'col'), may hold values from -0.125 to 0.125
Outputs:
- commands: bfloat16 [4, 1024, 4096], P(('row', 'dir'), 'grp', 'col'), parts along dimension 1
There are 2 independent parts, one for each index of `grp`. A program takes and returns all parts, laid end to end along the dimension named above; an argument that names none is the same for every part. Nothing has to cross between parts.
Inputs may be any that keep to these rules, and one draw needn't show every extreme that they name: rank_blocks[i, k] is the number of leading blocks of 64 columns of tile (i, k) that are live. `tile_owner`: each slope block appears in exactly one tile slot. `footprint`: indices into one layer's points.
All inputs are finite; a program needn't handle non-finite values.
Results may differ from a plain program's by a relative error of at most 0.0064.
Values may be sent and summed in bfloat16 or wider, within the bound.
No kernel may reach another device: no remote copies, remote signals or barrier semaphores. Data moves between devices by JAX's collectives and lax.ppermute only.
A program may use at most 128 MiB of HBM per device.

v0:
```python
import jax
import jax.numpy as jnp
from jax import lax
from jax.sharding import PartitionSpec as P

RB = 64


def shards(
    slopes_in, basis_left, basis_right, rank_blocks, tile_owner, footprint, trace_weight, fitting
):
    frames = slopes_in.shape[0]
    tile_size = basis_left.shape[2]
    rows_here = basis_left.shape[0]
    slots_here = basis_left.shape[1]
    rank_cols = basis_left.shape[3]
    owners = lax.dynamic_slice_in_dim(tile_owner, lax.axis_index("col") * slots_here, slots_here, 0)
    share = frames // lax.axis_size(("row", "dir"))
    mine = lax.dynamic_slice_in_dim(slopes_in, lax.axis_index(("row", "dir")) * share, share, 0)
    partial_value = lax.all_gather(mine, "col", axis=1, tiled=True)
    picked = jnp.take(partial_value.reshape(share, -1, tile_size), owners, axis=1)
    chosen = lax.all_gather(picked, ("row", "dir"), axis=0, tiled=True)
    columns = jnp.arange(rank_cols, dtype=jnp.int32) // RB
    live = columns[None, None, None, :] < rank_blocks[:, :, None, None]
    frame_share = frames // lax.axis_size("col")
    coeffs = jnp.einsum("fkn,iknr->ikfr", chosen, basis_right, preferred_element_type=jnp.float32)
    coeffs = jnp.where(live, coeffs, 0.0).astype(jnp.bfloat16)
    summed = jnp.einsum("ikfr,iknr->fin", coeffs, basis_left, preferred_element_type=jnp.float32)
    layer_block = lax.psum_scatter(
        summed.reshape(lax.axis_size("col") * frame_share, rows_here * tile_size),
        "col",
        scatter_dimension=0,
        tiled=True,
    ).astype(jnp.bfloat16)
    layers = lax.all_gather(layer_block, ("row", "dir"), axis=1, tiled=True)
    layer_count = footprint.shape[1]
    pupil_count = footprint.shape[3]
    per_layer = layers.shape[1] // layer_count
    shifts = (jnp.arange(layer_count, dtype=jnp.int32) * per_layer)[:, None, None]
    flat = (footprint[0] + shifts).reshape(-1)
    values = (
        jnp.take(layers, flat, axis=1)
        .astype(jnp.float32)
        .reshape(frame_share, layer_count, 4, pupil_count)
    )
    pupil = jnp.sum(values * trace_weight[0][None], axis=(1, 2)).astype(jnp.bfloat16)
    commands = jnp.dot(
        lax.all_gather(pupil, "col", axis=0, tiled=True),
        fitting,
        preferred_element_type=jnp.float32,
    )
    return commands.astype(jnp.bfloat16)[None]


def solution(mesh):
    placed = (
        P(None, ("grp", "col")),
        P(("row", "dir"), "col", None, None),
        P(("row", "dir"), "col", None, None),
        P(("row", "dir"), "col"),
        P(),
        P(("row", "dir"), None, None, None),
        P(("row", "dir"), None, None, None),
        P(None, "col"),
    )
    return jax.shard_map(
        shards,
        mesh=mesh,
        in_specs=placed,
        out_specs=P(("row", "dir"), "grp", "col"),
        check_vma=False,
    )
```

profile of v0, /device:TPU:0, one launch (start us, length us, event | category | flops | bytes accessed | tf_op | source)
XLA Modules:
  0.0 293.8 jit_solution(6185712206535708235)
XLA Ops:
  6.6 1.1 constant_dynamic-slice_fusion
  7.7 0.8 copy.14
  8.5 0.0 all-gather.6.cloned.1.call-start
  8.6 0.7 compare_and_fusion.1
  9.3 30.3 %all-gather.4.cloned.1.call-done = bf16[128,4096]{0,1:T(8,128)(2,1)} async-done(((bf16[128,1024]{0,1:T(8,128)(2,1)}), bf16[128,4096]{0,1:T(8,128)(2,1)}) %all-gather.4.cloned.1.call-update) | async-done | bytes 1048592 | tf_op jit(solution)/shard_map/all_gather | solution.py:20
  39.6 1.5 copy.12
  41.1 0.6 gather_fusion
  41.7 0.8 select_bitcast_fusion
  42.5 0.0 reduce-scatter.2.cloned.1.call-start
  42.6 0.1 add.67
  42.7 0.2 add.75
  42.9 0.2 squeeze.6
  43.1 0.1 broadcast_compare_fusion
  43.1 15.6 %all-gather.6.cloned.1.call-done = bf16[512,4,256]{2,0,1:T(8,128)(2,1)} async-done(((bf16[128,4,256]{2,0,1:T(8,128)(2,1)}), bf16[512,4,256]{2,0,1:T(8,128)(2,1)}) %all-gather.6.cloned.1.call-update) | async-done | bytes 1048592 | tf_op jit(solution)/shard_map/all_gather | solution.py:22
  58.8 4.7 %fusion.1 = f32[3,512,256,1]{1,2,3,0:T(8,128)} fusion(bf16[3,4,256,256]{3,2,1,0:T(8,128)(2,1)S(1)} %copy-done, pred[3,4,256]{2,1,0:T(4,128)(4,1)S(1)} %broadcast_compare_fusion, bf16[3,4,256,256]{3,2,1,0:T(8,128)(2,1)} %param.10, bf16[512,4,256]{2,0,1:T(8,128)(2,1)} %all-gather.6.cloned.1.call-done), kind=kOutput, calls=%fused_computation.5 | convolution fusion | flops 1613758464 | bytes 5770240 | tf_op jit(solution)/shard_map/ikfr,iknr->fin/dot_general | solution.py:28
  63.5 0.2 compare_select_fusion
  63.7 0.2 compare_and_fusion
  63.9 35.2 %reduce-scatter.2.cloned.1.call-done = f32[128,768]{0,1:T(8,128)} async-done(((f32[512,768]{0,1:T(8,128)}), f32[128,768]{0,1:T(8,128)}) %reduce-scatter.2.cloned.1.call-update) | async-done | bytes 393232 | tf_op jit(solution)/shard_map/reduce_scatter | solution.py:29
  99.1 1.0 convert_element_type.17
  100.1 8.6 %all_gather.14 = bf16[128,3072]{0,1:T(8,128)(2,1)S(1)} all-gather(bf16[128,768]{0,1:T(8,128)(2,1)S(1)} %convert_element_type.17), channel_id=1, replica_groups=mesh['grp'=2,'col'=4,'row'=2,'dir'=2] {'row','dir'}, dimensions={1}, use_global_device_ids=true | all-gather | bytes 983040 | tf_op jit(solution)/shard_map/all_gather | solution.py:35
  108.6 114.3 %gather_fusion.1 = bf16[32768,128]{1,0:T(8,128)(2,1)} fusion(bf16[128,3072]{0,1:T(8,128)(2,1)S(1)} %all_gather.14, s32[32768]{0:T(1024)S(1)} %broadcast_clamp_fusion), kind=kCustom, calls=%fused_computation.1 | custom fusion | bytes 16908288 | tf_op jit(solution)/shard_map/jit(_take)/gather | solution.py:42
  222.9 13.4 %multiply_reduce_fusion = bf16[128,2048]{0,1:T(8,128)(2,1)} fusion(f32[4,4,2048]{2,1,0:T(4,128)S(1)} %bitcast.39, bf16[128,4,4,2048]{0,3,2,1:T(8,128)(2,1)} %bitcast.35, pred[4,4,2048]{2,1,0:T(4,128)(4,1)S(1)} %compare_and_fusion), kind=kLoop, calls=%fused_computation.2 | loop fusion | flops 16515072 | bytes 9076736 | tf_op jit(solution)/shard_map/reduce_sum | solution.py:46
  236.3 44.8 %all-gather.8.cloned.1.call-done = bf16[512,2048]{0,1:T(8,128)(2,1)} async-done(((bf16[128,2048]{0,1:T(8,128)(2,1)}), bf16[512,2048]{0,1:T(8,128)(2,1)}) %all-gather.8.cloned.1.call-update) | async-done | bytes 2097168 | tf_op jit(solution)/shard_map/all_gather | solution.py:48
  281.2 6.1 %fusion.7 = bf16[1,512,1024]{2,1,0:T(8,128)(2,1)} fusion(bf16[512,2048]{0,1:T(8,128)(2,1)} %all-gather.8.cloned.1.call-done, bf16[2048,1024]{1,0:T(8,128)(2,1)} %param.15), kind=kOutput, calls=%fused_computation.10 | convolution fusion | flops 2148007936 | bytes 7340032 | tf_op jit(solution)/shard_map/dot_general | solution.py:47
  (18 shorter events, 0.2 us)
Async XLA Ops:
  6.5 52.2 %copy-start = (bf16[3,4,256,256]{3,2,1,0:T(8,128)(2,1)S(1)}, bf16[3,4,256,256]{3,2,1,0:T(8,128)(2,1)}, u32[]{:S(2)}) copy-start(bf16[3,4,256,256]{3,2,1,0:T(8,128)(2,1)} %param.9) | copy-start | bytes 4718596
  6.5 36.3 %copy-start.1 = (s32[1,4,4,2048]{3,2,1,0:T(4,128)S(1)}, s32[1,4,4,2048]{3,2,1,0:T(4,128)}, u32[]{:S(2)}) copy-start(s32[1,4,4,2048]{3,2,1,0:T(4,128)} %param.13) | copy-start | bytes 393220
  6.5 36.5 %copy-start.3 = (s32[3,4]{1,0:T(4,128)S(1)}, s32[3,4]{1,0:T(4,128)}, u32[]{:S(2)}) copy-start(s32[3,4]{1,0:T(4,128)} %param.11) | copy-start | bytes 148
  6.5 33.1 %all-gather.4.cloned.1.call-start = ((), (), s32[]{:S(2)}) async-start(), calls=%async_computation.1 | async-start | bytes 1310720 | tf_op jit(solution)/shard_map/all_gather | solution.py:20
  8.5 50.2 %all-gather.6.cloned.1.call-start = ((), (), s32[]{:S(2)}) async-start(), calls=%async_computation.2 | async-start | bytes 1310720 | tf_op jit(solution)/shard_map/all_gather | solution.py:22
  42.5 56.5 %reduce-scatter.2.cloned.1.call-start = ((), (), s32[]{:S(2)}) async-start(), calls=%async_computation.3 | async-start | bytes 1966080 | tf_op jit(solution)/shard_map/reduce_scatter | solution.py:29
  63.5 217.7 %all-gather.8.cloned.1.call-start = ((), (), s32[]{:S(2)}) async-start(), calls=%async_computation.4 | async-start | bytes 2621440 | tf_op jit(solution)/shard_map/all_gather | solution.py:48
  108.6 114.3 %copy-start.2 = (f32[1,4,4,2048]{3,2,1,0:T(4,128)S(1)}, f32[1,4,4,2048]{3,2,1,0:T(4,128)}, u32[]{:S(2)}) copy-start(f32[1,4,4,2048]{3,2,1,0:T(4,128)} %param.14) | copy-start | bytes 393220
Sparse Core Ops, SparseCore 0:
  8.9 30.6 all-gather.3
  42.6 16.0 all-gather.5
  63.6 35.4 reduce-scatter.1
  236.5 44.6 all-gather.7
where the time goes:
time: 294 us
  waiting for transfers between devices  126 us (43%)
  local copies, waits for them, and re-layouts  119 us (40%)
  other arithmetic  16.4 us (6%)
  between operations  13.2 us (4%)
  matrix products  10.8 us (4%)
  blocking collectives  8.58 us (3%)
    gather x1, local copies, waits for them, and re-layouts, shards(): jnp.take(layers, flat, axis=1).astype(jnp.float32)  114 us
    all_gather x1, waiting for transfers between devices, shards(): lax.all_gather(pupil, 'col', axis=0, tiled=True)  44.8 us
    reduce_scatter x1, waiting for transfers between devices, shards(): lax.psum_scatter(summed.reshape(lax.axis_size('col') * frame_share, rows_...  35.2 us
    all_gather x1, waiting for transfers between devices, shards(): partial_value = lax.all_gather(mine, 'col', axis=1, tiled=True)  30.3 us
    all_gather x1, waiting for transfers between devices, shards(): chosen = lax.all_gather(picked, ('row', 'dir'), axis=0, tiled=True)  15.6 us
    reduce_sum x1, other arithmetic, shards(): jnp.sum(values * trace_weight[0][None], axis=(1, 2)).astype(jnp.bfloat16)  13.4 us
    all_gather x1, blocking collectives, shards(): layers = lax.all_gather(layer_block, ('row', 'dir'), axis=1, tiled=True)  8.58 us
    dot_general x1, matrix products, shards(): jnp.dot(lax.all_gather(pupil, 'col', axis=0, tiled=True), fitting, prefer...  6.14 us
  transfers between devices with their start and end apart: 4, of which 4 were waited for; matrix products, arithmetic and copies ran while one was open for 1% of the time, Pallas kernels for 0%

commit v1 on v0

--- a/solution.py
+++ b/solution.py
@@ -4,6 +4,32 @@
 from jax.sharding import PartitionSpec as P
 
 RB = 64
+
+
+def on_each_block(value, axis, dim, work, out_dim):
+    size, mine, extent = (lax.axis_size(axis), lax.axis_index(axis), value.shape[dim])
+    right = [(i, (i + 1) % size) for i in range(size)]
+    left = [(b, a) for a, b in right]
+    lower, upper = (lax.ppermute(value, axis, right), lax.ppermute(value, axis, left))
+    made = work(value, mine * extent)
+    length = made.shape[out_dim]
+    filled = jnp.zeros(
+        (*made.shape[:out_dim], size * length, *made.shape[out_dim + 1 :]), made.dtype
+    )
+
+    def put(filled, made, owner):
+        return lax.dynamic_update_slice_in_dim(filled, made, owner * length, axis=out_dim)
+
+    filled = put(filled, made, mine)
+    for step in range(1, size // 2 + 1):
+        below, above = ((mine - step) % size, (mine + step) % size)
+        carried = (lower, upper)
+        if step < size // 2:
+            lower, upper = (lax.ppermute(lower, axis, right), lax.ppermute(upper, axis, left))
+        filled = put(filled, work(carried[0], below * extent), below)
+        if 2 * step < size:
+            filled = put(filled, work(carried[1], above * extent), above)
+    return filled
 
 
 def shards(
@@ -19,11 +45,18 @@
     mine = lax.dynamic_slice_in_dim(slopes_in, lax.axis_index(("row", "dir")) * share, share, 0)
     partial_value = lax.all_gather(mine, "col", axis=1, tiled=True)
     picked = jnp.take(partial_value.reshape(share, -1, tile_size), owners, axis=1)
-    chosen = lax.all_gather(picked, ("row", "dir"), axis=0, tiled=True)
     columns = jnp.arange(rank_cols, dtype=jnp.int32) // RB
     live = columns[None, None, None, :] < rank_blocks[:, :, None, None]
     frame_share = frames // lax.axis_size("col")
-    coeffs = jnp.einsum("fkn,iknr->ikfr", chosen, basis_right, preferred_element_type=jnp.float32)
+    coeffs = on_each_block(
+        picked,
+        ("row", "dir"),
+        0,
+        lambda part, at: jnp.einsum(
+            "fkn,iknr->ikfr", part, basis_right, preferred_element_type=jnp.float32
+        ),
+        2,
+    )
     coeffs = jnp.where(live, coeffs, 0.0).astype(jnp.bfloat16)
     summed = jnp.einsum("ikfr,iknr->fin", coeffs, basis_left, preferred_element_type=jnp.float32)
     layer_block = lax.psum_scatter(

time: 294 us -> 288 us (0.980)
  waiting for transfers between devices: 126 us -> 118 us
    all_gather x1 -> x0, waiting for transfers between devices: 15.6 us -> none  [shards(): chosen = lax.all_gather(picked, ('row', 'dir'), axis=0, tiled=True)]
    ppermute x0 -> x3, waiting for transfers between devices: none -> 9.37 us  [the longest x1 4.65 us: on_each_block(): lax.ppermute(lower, axis, right)]
  transfers between devices with their start and end apart: 4 -> 6, of which waited for: 4 -> 6; matrix products, arithmetic and copies ran while one was open for 1% -> 2% of each run, Pallas kernels for 0% -> 0%
where the time goes in v1:
time: 288 us
  local copies, waits for them, and re-layouts  120 us (42%)
  waiting for transfers between devices  118 us (41%)
  other arithmetic  16.4 us (6%)
  between operations  13.4 us (5%)
  matrix products  9.88 us (3%)
  blocking collectives  8.6 us (3%)
    gather x1, local copies, waits for them, and re-layouts, shards(): jnp.take(layers, flat, axis=1).astype(jnp.float32)  114 us
    all_gather x1, waiting for transfers between devices, shards(): lax.all_gather(pupil, 'col', axis=0, tiled=True)  44.8 us
    reduce_scatter x1, waiting for transfers between devices, shards(): lax.psum_scatter(summed.reshape(lax.axis_size('col') * frame_share, rows_...  35.4 us
    all_gather x1, waiting for transfers between devices, shards(): partial_value = lax.all_gather(mine, 'col', axis=1, tiled=True)  28.1 us
    reduce_sum x1, other arithmetic, shards(): jnp.sum(values * trace_weight[0][None], axis=(1, 2)).astype(jnp.bfloat16)  13.4 us
    all_gather x1, blocking collectives, shards(): layers = lax.all_gather(layer_block, ('row', 'dir'), axis=1, tiled=True)  8.6 us
    dot_general x1, matrix products, shards(): jnp.dot(lax.all_gather(pupil, 'col', axis=0, tiled=True), fitting, prefer...  6.14 us
  transfers between devices with their start and end apart: 6, of which 6 were waited for; matrix products, arithmetic and copies ran while one was open for 2% of the time, Pallas kernels for 0%

profile of v1, /device:TPU:0, one launch (start us, length us, event | category | flops | bytes accessed | tf_op | source)
XLA Modules:
  0.0 287.7 jit_solution(12868500627824646772)
XLA Ops:
  6.5 1.1 constant_dynamic-slice_fusion
  7.6 0.8 copy.14
  8.9 1.1 squeeze.6
  10.0 0.7 compare_and_fusion.1
  10.7 0.8 broadcast_compare_fusion
  11.5 28.1 %all-gather.3.cloned.1.call-done = bf16[128,4096]{0,1:T(8,128)(2,1)} async-done(((bf16[128,1024]{0,1:T(8,128)(2,1)}), bf16[128,4096]{0,1:T(8,128)(2,1)}) %all-gather.3.cloned.1.call-update) | async-done | bytes 1048592 | tf_op jit(solution)/shard_map/all_gather | solution.py:46
  39.6 1.5 copy.12
  41.1 0.6 gather_fusion
  41.9 1.7 collective-permute-start.1
  43.9 0.4 bitcast_dynamic-update-slice_fusion.3
  44.3 4.4 %collective-permute-done = bf16[128,4,256]{2,0,1:T(8,128)(2,1)S(1)} collective-permute-done((bf16[128,4,256]{2,0,1:T(8,128)(2,1)S(1)}, bf16[128,4,256]{2,0,1:T(8,128)(2,1)S(1)}, u32[]{:S(2)}, u32[]{:S(2)}) %collective-permute-start) | collective-permute-done | bytes 262176 | tf_op jit(solution)/shard_map/ppermute | solution.py:13
  48.7 0.4 bitcast_dynamic-update-slice_fusion.2
  49.1 0.3 collective-permute-done.1
  49.4 0.4 bitcast_dynamic-update-slice_fusion.1
  49.8 4.7 %collective-permute-done.2 = bf16[128,4,256]{2,0,1:T(8,128)(2,1)S(1)} collective-permute-done((bf16[128,4,256]{2,0,1:T(8,128)(2,1)S(1)}, bf16[128,4,256]{2,0,1:T(8,128)(2,1)S(1)}, u32[]{:S(2)}, u32[]{:S(2)}) %collective-permute-start.2) | collective-permute-done | bytes 262176 | tf_op jit(solution)/shard_map/ppermute | solution.py:28
  54.5 0.4 bitcast_dynamic-update-slice_fusion
  54.9 2.2 fusion
  57.5 35.4 %reduce-scatter.2.cloned.1.call-done = f32[128,768]{0,1:T(8,128)} async-done(((f32[512,768]{0,1:T(8,128)}), f32[128,768]{0,1:T(8,128)}) %reduce-scatter.2.cloned.1.call-update) | async-done | bytes 393232 | tf_op jit(solution)/shard_map/reduce_scatter | solution.py:62
  93.0 1.0 convert_element_type.17
  94.0 8.6 %all_gather.10 = bf16[128,3072]{0,1:T(8,128)(2,1)S(1)} all-gather(bf16[128,768]{0,1:T(8,128)(2,1)S(1)} %convert_element_type.17), channel_id=1, replica_groups=mesh['grp'=2,'col'=4,'row'=2,'dir'=2] {'row','dir'}, dimensions={1}, use_global_device_ids=true | all-gather | bytes 983040 | tf_op jit(solution)/shard_map/all_gather | solution.py:68
  102.6 114.2 %gather_fusion.1 = bf16[32768,128]{1,0:T(8,128)(2,1)} fusion(bf16[128,3072]{0,1:T(8,128)(2,1)S(1)} %all_gather.10, s32[32768]{0:T(1024)S(1)} %broadcast_clamp_fusion), kind=kCustom, calls=%fused_computation.1 | custom fusion | bytes 16908288 | tf_op jit(solution)/shard_map/jit(_take)/gather | solution.py:75
  216.8 13.4 %multiply_reduce_fusion = bf16[128,2048]{0,1:T(8,128)(2,1)} fusion(f32[4,4,2048]{2,1,0:T(4,128)S(1)} %bitcast.54, bf16[128,4,4,2048]{0,3,2,1:T(8,128)(2,1)} %bitcast.50, pred[4,4,2048]{2,1,0:T(4,128)(4,1)S(1)} %compare_and_fusion), kind=kLoop, calls=%fused_computation.2 | loop fusion | flops 16515072 | bytes 9076736 | tf_op jit(solution)/shard_map/reduce_sum | solution.py:79
  230.2 44.8 %all-gather.5.cloned.1.call-done = bf16[512,2048]{0,1:T(8,128)(2,1)} async-done(((bf16[128,2048]{0,1:T(8,128)(2,1)}), bf16[512,2048]{0,1:T(8,128)(2,1)}) %all-gather.5.cloned.1.call-update) | async-done | bytes 2097168 | tf_op jit(solution)/shard_map/all_gather | solution.py:81
  275.0 6.1 %fusion.3 = bf16[1,512,1024]{2,1,0:T(8,128)(2,1)} fusion(bf16[512,2048]{0,1:T(8,128)(2,1)} %all-gather.5.cloned.1.call-done, bf16[2048,1024]{1,0:T(8,128)(2,1)} %param.15), kind=kOutput, calls=%fused_computation.12 | convolution fusion | flops 2148007936 | bytes 7340032 | tf_op jit(solution)/shard_map/dot_general | solution.py:80
  (26 shorter events, 1.2 us)
Async XLA Ops:
  6.5 37.3 %copy-start = (bf16[3,4,256,256]{3,2,1,0:T(8,128)(2,1)S(1)}, bf16[3,4,256,256]{3,2,1,0:T(8,128)(2,1)}, u32[]{:S(2)}) copy-start(bf16[3,4,256,256]{3,2,1,0:T(8,128)(2,1)} %param.10) | copy-start | bytes 4718596
  6.5 33.1 %all-gather.3.cloned.1.call-start = ((), (), s32[]{:S(2)}) async-start(), calls=%async_computation.1 | async-start | bytes 1310720 | tf_op jit(solution)/shard_map/all_gather | solution.py:46
  8.5 84.5 %reduce-scatter.2.cloned.1.call-start = ((), (), s32[]{:S(2)}) async-start(), calls=%async_computation.2 | async-start | bytes 1966080 | tf_op jit(solution)/shard_map/reduce_scatter | solution.py:62
  41.8 6.9 %collective-permute-start = (bf16[128,4,256]{2,0,1:T(8,128)(2,1)S(1)}, bf16[128,4,256]{2,0,1:T(8,128)(2,1)S(1)}, u32[]{:S(2)}, u32[]{:S(2)}) collective-permute-start(bf16[128,4,256]{2,0,1:T(8,128)(2,1)S(1)} %fusion.8), channel_id=1, source_target_pairs={{0,1},{1,2},{2,3},{3,0},{4,5},{5,6},{6,7},{7,4},{8,9},{9,10},{10,1... | collective-permute-start | bytes 786440 | tf_op jit(solution)/shard_map/ppermute | solution.py:13
  41.9 7.6 %collective-permute-start.1 = (bf16[128,4,256]{2,0,1:T(8,128)(2,1)S(1)}, bf16[128,4,256]{2,0,1:T(8,128)(2,1)S(1)}, u32[]{:S(2)}, u32[]{:S(2)}) collective-permute-start(bf16[128,4,256]{2,0,1:T(8,128)(2,1)S(1)} %fusion.8), channel_id=1, source_target_pairs={{1,0},{2,1},{3,2},{0,3},{5,4},{6,5},{7,6},{4,7},{9,8},{10,9},{11,1... | collective-permute-start | bytes 786440 | tf_op jit(solution)/shard_map/ppermute | solution.py:13
  48.7 5.8 %collective-permute-start.2 = (bf16[128,4,256]{2,0,1:T(8,128)(2,1)S(1)}, bf16[128,4,256]{2,0,1:T(8,128)(2,1)S(1)}, u32[]{:S(2)}, u32[]{:S(2)}) collective-permute-start(bf16[128,4,256]{2,0,1:T(8,128)(2,1)S(1)} %collective-permute-done), channel_id=1, source_target_pairs={{0,1},{1,2},{2,3},{3,0},{4,5},{5,6},{6,7},{7,4},{8,9},{9,10},{10,1... | collective-permute-start | bytes 786440 | tf_op jit(solution)/shard_map/ppermute | solution.py:28
  49.1 5.8 %copy-start.3 = (bf16[3,4,256,256]{3,2,1,0:T(8,128)(2,1)S(1)}, bf16[3,4,256,256]{3,2,1,0:T(8,128)(2,1)}, u32[]{:S(2)}) copy-start(bf16[3,4,256,256]{3,2,1,0:T(8,128)(2,1)} %param.9) | copy-start | bytes 4718596
  54.9 2.4 copy-start.1
  57.1 217.9 %all-gather.5.cloned.1.call-start = ((), (), s32[]{:S(2)}) async-start(), calls=%async_computation.3 | async-start | bytes 2621440 | tf_op jit(solution)/shard_map/all_gather | solution.py:81
  102.6 114.2 %copy-start.2 = (f32[1,4,4,2048]{3,2,1,0:T(4,128)S(1)}, f32[1,4,4,2048]{3,2,1,0:T(4,128)}, u32[]{:S(2)}) copy-start(f32[1,4,4,2048]{3,2,1,0:T(4,128)} %param.14) | copy-start | bytes 393220
Sparse Core Ops, SparseCore 0:
  8.9 30.6 all-gather.2
  57.2 35.6 reduce-scatter.1
  230.3 44.6 all-gather.4
